TPU v7x, 32 devices: a whole 2x2x4 slice. The times are simulated.
32 devices in a mesh: seq: 4 (over z), head: 2 (over core), batch: 4 (over y, x).
Axes of the slice: x: 2, y: 2, z: 4, core: 2. Of those that a mesh axis runs over, the one named last changes fastest.
Arguments:
- queries: bfloat16 [16384, 8, 256], P(('batch', 'seq'), 'head'), parts along dimension 0, may hold values from -6 to 6
- keys: bfloat16 [16384, 8, 256], P(('batch', 'seq'), 'head'), parts along dimension 0, may hold values from -0.375 to 0.375
- content_vectors: bfloat16 [16384, 8, 256], P(('batch', 'seq'), 'head'), parts along dimension 0, may hold values from -6 to 6
- decay_rate: float32 [8, 16384], P('head', ('batch', 'seq')), parts along dimension 1, may hold values from 0 to 3
- gate_pre: bfloat16 [16384, 2048], P(('batch', 'seq'), 'head'), parts along dimension 0, may hold values from -6 to 6
- norm_gain: float32 [2048], P('head'), may hold values from 0.1 to 1.9
- out_weight: bfloat16 [2048, 4096], P('head'), may hold values from -0.125 to 0.125
Outputs:
- layer_out: bfloat16 [16384, 4096], P(('batch', 'seq'), 'head'), parts along dimension 0
There are 4 independent parts, one for each index of `batch`. A program takes and returns all parts, laid end to end along the dimension named above; an argument that names none is the same for every part. Nothing has to cross between parts.
All inputs are finite; a program needn't handle non-finite values.
Results may differ from a plain program's by a relative error of at most 0.013.
Values may be sent and summed in bfloat16 or wider, within the bound.
A program may use at most 128 MiB of HBM per device.

v0:
```python
import jax
import jax.numpy as jnp
from jax import lax
from jax.sharding import PartitionSpec as P


def transpose_prefix(totals, segment_retained_matrix):
    devices = lax.axis_size("seq")
    every_total = lax.all_gather(totals[None, :], "seq", axis=0, tiled=True)
    before = jnp.cumsum(every_total, axis=0) - every_total
    target = jnp.arange(devices)[:, None]
    source = jnp.arange(devices)[None, :]
    exponent = before.T[:, :, None] - before.T[:, None, :] - every_total.T[:, None, :]
    factors = jnp.exp(jnp.where((source < target)[None], exponent, -jnp.inf))
    aggregate_result = jnp.einsum(
        "hde,herv->hdrv",
        factors,
        lax.all_to_all(
            segment_retained_matrix[:, None], "seq", split_axis=2, concat_axis=1, tiled=True
        ),
        precision=lax.Precision.HIGHEST,
    )
    gathered = lax.all_to_all(
        aggregate_result.astype(jnp.bfloat16), "seq", split_axis=1, concat_axis=2, tiled=True
    ).astype(aggregate_result.dtype)
    return gathered[:, 0]


def on_device(queries, keys, content_vectors, decay_rate, gate_pre, norm_gain, out_weight):
    length = queries.shape[0]
    local_heads = queries.shape[1]
    value_width = content_vectors.shape[2]
    within = -jnp.cumsum(decay_rate, axis=1)
    totals = within[:, -1]
    lookup_vectors_weighted = (jnp.exp(totals[None, :] - within.T)[:, :, None] * keys).astype(
        jnp.bfloat16
    )
    segment_retained_matrix = jnp.einsum(
        "gdj,gdl->djl", lookup_vectors_weighted, content_vectors, preferred_element_type=jnp.float32
    )
    arriving_state = transpose_prefix(totals, segment_retained_matrix)
    arriving_state_rounded = arriving_state.astype(jnp.bfloat16)
    passed_forward = jnp.einsum(
        "qaw,awi->qai", queries, arriving_state_rounded, preferred_element_type=jnp.float32
    )
    passed_forward = passed_forward * jnp.exp(within.T)[:, :, None]
    scores = jnp.einsum("lhk,shk->hls", queries, keys, preferred_element_type=jnp.float32)
    token_positions = jnp.arange(length)
    causal = token_positions[:, None] >= token_positions[None, :]
    exponent = jnp.where(causal[None], within[:, :, None] - within[:, None, :], -jnp.inf)
    weights = (scores * jnp.exp(exponent)).astype(jnp.bfloat16)
    within_block = jnp.einsum(
        "hls,shv->lhv", weights, content_vectors, preferred_element_type=jnp.float32
    )
    retained = passed_forward + within_block
    center = jnp.mean(retained, axis=2, keepdims=True)
    shifted = retained - center
    variance = jnp.mean(shifted * shifted, axis=2, keepdims=True)
    normed = (shifted * lax.rsqrt(variance + 1e-06)).reshape(length, local_heads * value_width)
    gated_rows = (normed * norm_gain * jax.nn.silu(gate_pre.astype(jnp.float32))).astype(
        jnp.bfloat16
    )
    partial_out = jnp.dot(gated_rows, out_weight, preferred_element_type=jnp.float32)
    result = lax.psum_scatter(
        partial_out.astype(jnp.bfloat16), "head", scatter_dimension=1, tiled=True
    )
    return result


def solution(mesh):
    in_specs = (
        P(("batch", "seq"), "head", None),
        P(("batch", "seq"), "head", None),
        P(("batch", "seq"), "head", None),
        P("head", ("batch", "seq")),
        P(("batch", "seq"), "head"),
        P("head"),
        P("head", None),
    )
    out_specs = P(("batch", "seq"), "head")
    return jax.shard_map(
        on_device, mesh=mesh, in_specs=in_specs, out_specs=out_specs, check_vma=False
    )
```

profile of v0, /device:TPU:27, one launch (start us, length us, event | category | flops | bytes accessed | tf_op | source)
XLA Modules:
  0.0 122.9 jit_solution(2913330382847279531)
XLA Ops:
  6.5 0.0 copy-start
  6.5 0.9 copy.96
  7.4 1.1 reduce-window.6
  8.5 0.2 slice_reduce_fusion
  8.7 0.2 reduce-window.9
  8.9 0.1 negate_bitcast_fusion
  9.0 0.1 slice.13
  9.0 0.1 copy.70
  9.1 0.1 exponential_bitcast_fusion
  9.2 0.2 copy.52
  9.5 4.3 %copy.64 = bf16[1024,4,256]{0,2,1:T(8,128)(2,1)} copy(bf16[1024,4,256]{2,1,0:T(4,128)(2,1)} %param.9) | data formatting | bytes 4194304 | tf_op args[2]
  13.8 0.0 copy-done
  13.8 0.0 copy-start.1
  13.8 2.4 %multiply_convert_fusion.1 = bf16[1024,4,256]{2,1,0:T(4,128)(2,1)S(1)} fusion(bf16[1024,4,256]{2,1,0:T(4,128)(2,1)S(1)} %copy-done, f32[1024,4]{1,0:T(8,128)S(1)} %copy.52), kind=kLoop, calls=%fused_computation.12 | loop fusion | flops 3145728 | bytes 4210688 | tf_op jit(solution)/shard_map/convert_element_type | solution.py:35
  16.3 0.0 copy-done.1
  16.3 0.0 copy-start.4
  16.3 0.9 fusion.16
  17.2 1.6 %copy.55 = f32[4,1,256,256]{3,0,1,2:T(4,128)} copy(f32[4,1,256,256]{3,2,0,1:T(8,128)S(1)} %fusion.16) | data formatting | bytes 2097152 | tf_op jit(solution)/shard_map/broadcast_in_dim | solution.py:19
  18.9 4.5 %all-to-all-start = ((f32[4,1,256,256]{3,0,1,2:T(4,128)}), f32[4,1,256,256]{3,0,1,2:T(4,128)S(1)}, u32[]{:S(2)}, u32[]{:S(2)}) async-start(f32[4,1,256,256]{3,0,1,2:T(4,128)} %copy.55), calls=%async_computation | async-start | bytes 2097152 | tf_op jit(solution)/shard_map/all_to_all | solution.py:18
  23.4 0.0 copy-done.4
  23.4 0.6 dynamic-slice
  24.6 0.1 bitcast_dynamic-update-slice_fusion
  24.7 23.0 %all-reduce = f32[16]{0:T(128)S(1)} all-reduce(f32[16]{0:T(128)S(1)} %bitcast_dynamic-update-slice_fusion), channel_id=2, replica_groups=mesh['seq'=4,'head'=2,'batch'=4] {'seq'}, use_global_device_ids=true, to_apply=%add | all-reduce | flops 16 | bytes 128
  47.7 0.1 reshape.90
  47.9 0.1 copy.51
  48.0 0.1 copy.49
  48.1 1.3 %iota_compare_fusion = pred[1024,1024]{1,0:T(8,128)(4,1)} fusion(), kind=kLoop, calls=%fused_computation.11 | loop fusion | flops 1048576 | bytes 1048576 | tf_op jit(solution)/shard_map/ge | solution.py:49
  49.4 0.0 all-to-all-done
  49.4 2.4 %convolution_convert_fusion.1 = bf16[4,4,64,256]{3,1,2,0:T(4,128)(2,1)S(1)} fusion(f32[4,4,64,256]{3,0,2,1:T(4,128)S(1)} %bitcast.45, f32[4,4]{1,0:T(4,128)S(1)} %copy.51, f32[4,4]{1,0:T(4,128)S(1)} %copy.49, pred[4,4]{1,0:T(4,128)(4,1)S(1)} %iota_compare_fusion.1), kind=kOutput, calls=%fused_computation.24 | convolution fusion | flops 12845248 | bytes 1573008 | tf_op jit(solution)/shard_map/hde,herv->hdrv/dot_general | solution.py:15
  51.7 0.9 copy.58
  52.6 4.6 %all-to-all-start.1 = ((bf16[4,4,64,256]{3,2,0,1:T(8,128)(2,1)}), bf16[4,4,64,256]{3,2,0,1:T(8,128)(2,1)S(1)}, u32[]{:S(2)}, u32[]{:S(2)}) async-start(bf16[4,4,64,256]{3,2,0,1:T(8,128)(2,1)} %copy.58), calls=%async_computation.1 | async-start | bytes 1048576 | tf_op jit(solution)/shard_map/all_to_all | solution.py:23
  57.3 0.0 reduce-scatter.2.cloned.1.call-start
  57.3 10.7 %fusion.5 = f32[4,1024,256]{1,2,0:T(8,128)} fusion(bf16[1024,4,256]{0,2,1:T(8,128)(2,1)} %copy.64, f32[4,1024]{1,0:T(4,128)S(1)} %bitcast.50, pred[1024,1024]{1,0:T(8,128)(4,1)} %iota_compare_fusion, bf16[1024,4,256]{2,1,0:T(4,128)(2,1)S(1)} %copy-done, bf16[1024,4,256]{2,1,0:T(4,128)(2,1)} %param.7), kind=kOutput, calls=%fused_computation.15 | convolution fusion | flops 4311744512 | bytes 11550720 | tf_op jit(solution)/shard_map/hls,shv->lhv/dot_general | solution.py:52
  68.0 0.5 all-to-all-done.1
  68.5 3.9 %fusion.33 = (f32[1024,4]{0,1:T(4,128)S(1)}, f32[1024,4,256]{0,2,1:T(8,128)S(1)}) fusion(f32[4,1024,256]{1,2,0:T(8,128)} %fusion.5, f32[1024,4]{0,1:T(4,128)S(1)} %get-tuple-element.5, bf16[4,256,256]{2,1,0:T(8,128)(2,1)S(1)} %bitcast.46, bf16[1024,4,256]{2,1,0:T(4,128)(2,1)} %param.7), kind=kOutput, calls=%fused_computation.50 | convolution fusion | flops 540012544 | bytes 11042816 | tf_op jit(solution)/shard_map/qaw,awi->qai/dot_general | solution.py:43
  72.4 0.5 multiply_reduce_fusion
  73.0 2.5 %subtract_multiply_fusion = f32[1024,4,256]{0,2,1:T(8,128)} fusion(f32[1024,4,256]{0,2,1:T(8,128)S(1)} %get-tuple-element.8, f32[1024,4]{0,1:T(4,128)S(1)} %add_rsqrt_fusion, f32[1024,4]{0,1:T(4,128)S(1)} %broadcast_multiply_fusion), kind=kLoop, calls=%fused_computation.14 | loop fusion | flops 2097152 | bytes 8421376 | tf_op jit(solution)/shard_map/mul | solution.py:59
  75.6 0.0 copy-start.2
  75.6 0.0 copy-start.3
  75.6 5.5 %copy.65 = f32[1024,1024]{1,0:T(8,128)} copy(f32[1024,1024]{0,1:T(8,128)} %bitcast.44) | data formatting | bytes 8388608 | tf_op jit(solution)/shard_map/reshape | solution.py:59
  81.1 0.0 copy-done.2
  81.1 0.0 copy-done.3
  81.1 15.0 %convolution_convert_fusion = bf16[1024,4096]{1,0:T(8,128)(2,1)} fusion(bf16[1024,4096]{1,0:T(8,128)(2,1)} %param.13, bf16[1024,1024]{1,0:T(8,128)(2,1)S(1)} %copy-done.2, f32[1024,1024]{1,0:T(8,128)} %copy.65, f32[1024]{0:T(1024)S(1)} %copy-done.3), kind=kOutput, calls=%fused_computation.1 | convolution fusion | flops 8602517504 | bytes 23072768 | tf_op jit(solution)/shard_map/dot_general | solution.py:63
  96.1 0.0 reduce-scatter.2.cloned.1.call-update
  96.1 20.0 %reduce-scatter.2.cloned.1.call-done = bf16[1024,2048]{1,0:T(8,128)(2,1)} async-done(((bf16[1024,4096]{1,0:T(8,128)(2,1)}), bf16[1024,2048]{1,0:T(8,128)(2,1)}) %reduce-scatter.2.cloned.1.call-update) | async-done | bytes 4194320 | tf_op jit(solution)/shard_map/reduce_scatter | solution.py:64
  (8 shorter events, 0.1 us)
Async XLA Ops:
  6.5 7.3 %copy-start = (bf16[1024,4,256]{2,1,0:T(4,128)(2,1)S(1)}, bf16[1024,4,256]{2,1,0:T(4,128)(2,1)}, u32[]{:S(2)}) copy-start(bf16[1024,4,256]{2,1,0:T(4,128)(2,1)} %param.8) | copy-start | bytes 6291460
  13.8 2.4 %copy-start.1 = (bf16[1024,4,256]{0,2,1:T(8,128)(2,1)S(1)}, bf16[1024,4,256]{0,2,1:T(8,128)(2,1)}, u32[]{:S(2)}) copy-start(bf16[1024,4,256]{0,2,1:T(8,128)(2,1)} %copy.64) | copy-start | bytes 6291460
  16.3 7.1 %copy-start.4 = (u32[32]{0:T(128)S(1)}, u32[32]{0:T(128)}, u32[]{:S(2)}) copy-start(u32[32]{0:T(128)} %constant.21) | copy-start | bytes 388
  18.9 30.5 %all-to-all-start = ((f32[4,1,256,256]{3,0,1,2:T(4,128)}), f32[4,1,256,256]{3,0,1,2:T(4,128)S(1)}, u32[]{:S(2)}, u32[]{:S(2)}) async-start(f32[4,1,256,256]{3,0,1,2:T(4,128)} %copy.55), calls=%async_computation | async-start | bytes 2097152 | tf_op jit(solution)/shard_map/all_to_all | solution.py:18
  52.6 15.9 %all-to-all-start.1 = ((bf16[4,4,64,256]{3,2,0,1:T(8,128)(2,1)}), bf16[4,4,64,256]{3,2,0,1:T(8,128)(2,1)S(1)}, u32[]{:S(2)}, u32[]{:S(2)}) async-start(bf16[4,4,64,256]{3,2,0,1:T(8,128)(2,1)} %copy.58), calls=%async_computation.1 | async-start | bytes 1048576 | tf_op jit(solution)/shard_map/all_to_all | solution.py:23
  57.3 58.8 %reduce-scatter.2.cloned.1.call-start = ((), (), s32[]{:S(2)}) async-start(), calls=%async_computation.3 | async-start | bytes 12582912 | tf_op jit(solution)/shard_map/reduce_scatter | solution.py:64
  75.6 5.5 %copy-start.2 = (bf16[1024,1024]{1,0:T(8,128)(2,1)S(1)}, bf16[1024,1024]{1,0:T(8,128)(2,1)}, u32[]{:S(2)}) copy-start(bf16[1024,1024]{1,0:T(8,128)(2,1)} %param.11) | copy-start | bytes 6291460
  75.6 5.5 %copy-start.3 = (f32[1024]{0:T(1024)S(1)}, f32[1024]{0:T(1024)}, u32[]{:S(2)}) copy-start(f32[1024]{0:T(1024)} %param.12) | copy-start | bytes 12292
Sparse Core Ops, SparseCore 0:
  96.2 19.8 reduce-scatter.1
where the time goes:
time: 124 us; the launch traced here: 123 us
  matrix products  32.9 us (27%)
  blocking collectives  23 us (19%)
  waiting for transfers between devices  20.5 us (17%)
  local copies, waits for them, and re-layouts  14.8 us (12%)
  between operations  14.1 us (11%)
  starting transfers between devices  9.18 us (7%)
  other arithmetic  8.36 us (7%)
    unnamed x1, blocking collectives  23 us
    reduce_scatter x1, waiting for transfers between devices, on_device(): lax.psum_scatter(partial_out.astype(jnp.bfloat16), 'head', scatter_dimens...  20 us
    dot_general x1, matrix products, on_device(): jnp.dot(gated_rows, out_weight, preferred_element_type=jnp.float32)  15 us
    dot_general x1, matrix products, on_device(): jnp.einsum('hls,shv->lhv', weights, content_vectors, preferred_element_ty...  10.7 us
    unnamed x17, local copies, waits for them, and re-layouts  6.03 us
    reshape x1, local copies, waits for them, and re-layouts, on_device(): (shifted * lax.rsqrt(variance + 1e-06)).reshape(length, local_heads * val...  5.49 us
    all_to_all x1, starting transfers between devices, transpose_prefix(): lax.all_to_all(aggregate_result.astype(jnp.bfloat16), 'seq', split_axis=1...  4.65 us
    all_to_all x1, starting transfers between devices, transpose_prefix(): lax.all_to_all(segment_retained_matrix[:, None], 'seq', split_axis=2, con...  4.53 us
  transfers between devices with their start and end apart: 3, of which 2 were waited for; matrix products, arithmetic and copies ran while one was open for 11% of the time, Pallas kernels for 0%

commit v1 on v0

v1 whole, which is shorter than its diff:
```python
import functools

import jax
import jax.numpy as jnp
from jax import lax
from jax.experimental import pallas as pl
from jax.experimental.pallas import tpu as pltpu
from jax.sharding import PartitionSpec as P

MESH = pl.DeviceIdType.MESH
SUB = 4
AHEAD = 6
LAG = 2 * SUB + 1


def kernel(
    blocks, q_hbm, k_hbm, v_hbm, rate_ref, gate_hbm, gain_ref, w_hbm, out_hbm,
    qv, kv, vv, gv, w_own, w_peer, g_own, g_peer, acc, ob, near, st, inc, sb,
    wrow, wcol, ecol, fstart, ftot,
    k_sem, v_sem, q_sem, gate_sem, w_sem, ws_sem, wr_sem, ss_sem, sr_sem, gs_sem, gr_sem, o_sem,
):
    length, dk = qv.shape[0], inc.shape[1]
    dv = inc.shape[2]
    heads = inc.shape[0]
    rows = length // SUB
    part = dk // SUB
    half = w_own.shape[1]
    tiles, _, width = acc.shape
    per = tiles // SUB
    s = lax.axis_index("seq")
    p = lax.axis_index("head")

    def k_copy(h):
        c = pl.ds(h * dk, dk)
        return pltpu.make_async_copy(k_hbm.at[:, c], kv.at[:, c], k_sem.at[h])

    def v_copy(h):
        c = pl.ds(h * dv, dv)
        return pltpu.make_async_copy(v_hbm.at[:, c], vv.at[:, c], v_sem.at[h])

    def w_local():
        c = pl.ds(pl.multiple_of(p * half, 128), half)
        return pltpu.make_async_copy(w_hbm.at[:, c], w_own, w_sem)

    def w_remote():
        c = pl.ds(pl.multiple_of((1 - p) * half, 128), half)
        return pltpu.make_async_remote_copy(
            w_hbm.at[:, c], w_peer, ws_sem, wr_sem,
            device_id={"head": 1 - p}, device_id_type=MESH,
        )

    def state_copy(h, j):
        c = pl.ds(pl.multiple_of(j * part, part), part)
        i = h * SUB + j
        return pltpu.make_async_remote_copy(
            sb.at[h, c], inc.at[h, c], ss_sem.at[i], sr_sem.at[i],
            device_id={"seq": lax.rem(s + 1, blocks)}, device_id_type=MESH,
        )

    def g_copy(h, r):
        c = pl.ds(pl.multiple_of(r * rows, rows), rows)
        i = h * SUB + r
        return pltpu.make_async_remote_copy(
            g_own.at[h, c], g_peer.at[h, c], gs_sem.at[i], gr_sem.at[i],
            device_id={"head": 1 - p}, device_id_type=MESH,
        )

    def out_copy(n):
        c = pl.ds(pl.multiple_of(n * width, width), width)
        return pltpu.make_async_copy(ob.at[n], out_hbm.at[:, c], o_sem.at[n])

    for h in range(heads):
        k_copy(h).start()
        v_copy(h).start()
    q_copy = pltpu.make_async_copy(q_hbm, qv, q_sem)
    gate_copy = pltpu.make_async_copy(gate_hbm, gv, gate_sem)
    q_copy.start()
    gate_copy.start()
    w_local().start()

    barrier = pltpu.get_barrier_semaphore()
    for there in (
        {"seq": lax.rem(s + 1, blocks)},
        {"seq": lax.rem(s + blocks - 1, blocks)},
        {"head": 1 - p},
    ):
        pl.semaphore_signal(barrier, inc=1, device_id=there, device_id_type=MESH)

    run = rate_ref[...]
    run = jnp.concatenate([run, run], axis=0)
    lane = lax.broadcasted_iota(jnp.int32, run.shape, 1)
    shift = 1
    while shift < length:
        run = run + jnp.where(lane >= shift, pltpu.roll(run, shift, 1), 0.0)
        shift *= 2
    within = -run
    columns = within.T
    for h in range(heads):
        wrow[h] = within[h : h + 1]
        wcol[h] = columns[:, h : h + 1]

    pl.semaphore_wait(barrier, 3)
    w_remote().start()

    @pl.when(s == 0)
    def _():
        inc[...] = jnp.zeros_like(inc)

    for h in range(heads):
        k_copy(h).wait()
        v_copy(h).wait()
        state = jnp.zeros((dk, dv), jnp.float32)
        start = jnp.zeros((1, 1), jnp.float32)
        for r in range(SUB):
            t = slice(r * rows, (r + 1) * rows)
            w = columns[t, h : h + 1]
            end = within[h : h + 1, (r + 1) * rows - 1 : (r + 1) * rows]
            ecol[h, t] = jnp.exp(w - start)
            fstart[h * SUB + r] = jnp.broadcast_to(jnp.exp(start), (1, dv))
            st[h * (SUB + 1) + r] = state
            scaled = (jnp.exp(end - w) * kv[t, h * dk : (h + 1) * dk]).astype(jnp.bfloat16)
            added = lax.dot_general(
                scaled, vv[t, h * dv : (h + 1) * dv], (((0,), (0,)), ((), ())),
                preferred_element_type=jnp.float32,
            )
            state = jnp.exp(end - start) * state + added
            start = end
        ftot[h] = jnp.broadcast_to(jnp.exp(start), (1, dv))
        st[h * (SUB + 1) + SUB] = state

        @pl.when(s == 0)
        def _():
            sb[h] = state.astype(jnp.bfloat16)
            for j in range(SUB):
                state_copy(h, j).start()

    q_copy.wait()
    gate_copy.wait()
    steps = heads * SUB
    lead = jnp.minimum(AHEAD * s, steps)

    def step(i, carry):
        @pl.when(i < steps)
        def _():
            h, r = i // SUB, lax.rem(i, SUB)
            t = pl.ds(pl.multiple_of(r * rows, rows), rows)
            ck = pl.ds(pl.multiple_of(h * dk, dk), dk)
            cv = pl.ds(pl.multiple_of(h * dv, dv), dv)
            scores = lax.dot_general(
                qv[t, ck], kv[t, ck], (((1,), (1,)), ((), ())), preferred_element_type=jnp.float32
            )
            y = lax.broadcasted_iota(jnp.int32, (rows, rows), 0)
            x = lax.broadcasted_iota(jnp.int32, (rows, rows), 1)
            gap = jnp.where(y >= x, wcol[h, t] - wrow[h, :, t], -jnp.inf)
            weights = (scores * jnp.exp(gap)).astype(jnp.bfloat16)
            near[h, t] = jnp.dot(weights, vv[t, cv], preferred_element_type=jnp.float32)

        c = i - lead

        @pl.when((c >= 0) & (c < steps) & (s > 0))
        def _():
            h, j = c // SUB, lax.rem(c, SUB)
            state_copy(h, j).wait_recv()

            @pl.when(s < blocks - 1)
            def _():
                t = pl.ds(pl.multiple_of(j * part, part), part)
                total = ftot[h] * inc[h, t].astype(jnp.float32) + st[h * (SUB + 1) + SUB, t]
                sb[h, t] = total.astype(jnp.bfloat16)
                state_copy(h, j).start()

        f = c - SUB

        @pl.when((f >= 0) & (f < steps))
        def _():
            h, r = f // SUB, lax.rem(f, SUB)
            t = pl.ds(pl.multiple_of(r * rows, rows), rows)
            ck = pl.ds(pl.multiple_of(h * dk, dk), dk)
            cv = pl.ds(pl.multiple_of(h * dv, dv), dv)
            state = st[h * (SUB + 1) + r] + fstart[h * SUB + r] * inc[h].astype(jnp.float32)
            far = jnp.dot(
                qv[t, ck], state.astype(jnp.bfloat16), preferred_element_type=jnp.float32
            )
            kept = near[h, t] + ecol[h, t] * far
            kept = kept - jnp.mean(kept, axis=1, keepdims=True)
            var = jnp.mean(kept * kept, axis=1, keepdims=True)
            g = gv[t, cv].astype(jnp.float32)
            gated = kept * lax.rsqrt(var + 1e-06) * gain_ref[:, cv] * (g / (1.0 + jnp.exp(-g)))
            g_own[h, t] = gated.astype(jnp.bfloat16)
            g_copy(h, r).start()

        o = c - LAG

        @pl.when(o == 0)
        def _():
            w_local().wait()
            w_remote().wait_recv()

        @pl.when((o >= 0) & (lax.rem(o, SUB) == 0))
        def _():
            for r in range(SUB):
                g_copy(o // SUB, r).wait_recv()

        @pl.when(o >= 0)
        def _():
            h = o // SUB
            ch = pl.ds(pl.multiple_of(h * dv, dv), dv)
            for u in range(per):
                n = lax.rem(o, SUB) * per + u
                cn = pl.ds(pl.multiple_of(n * width, width), width)
                total = jnp.dot(g_own[h], w_own[ch, cn], preferred_element_type=jnp.float32)
                total += jnp.dot(g_peer[h], w_peer[ch, cn], preferred_element_type=jnp.float32)

                @pl.when(h == 0)
                def _():
                    acc[n] = total

                @pl.when((h > 0) & (h < heads - 1))
                def _():
                    acc[n] += total

                @pl.when(h == heads - 1)
                def _():
                    ob[n] = (acc[n] + total).astype(jnp.bfloat16)
                    out_copy(n).start()

        return carry

    lax.fori_loop(0, lead + steps + LAG, step, 0)

    w_remote().wait_send()

    def finish(i, carry):
        g_copy(i // SUB, lax.rem(i, SUB)).wait_send()

        @pl.when(s < blocks - 1)
        def _():
            state_copy(i // SUB, lax.rem(i, SUB)).wait_send()

        return carry

    lax.fori_loop(0, steps, finish, 0)
    for n in range(tiles):
        out_copy(n).wait()


def on_device(queries, keys, content_vectors, decay_rate, gate_pre, norm_gain, out_weight):
    length, heads, dk = queries.shape
    dv = content_vectors.shape[2]
    blocks = lax.axis_size("seq")
    half = out_weight.shape[1] // lax.axis_size("head")
    tiles = 2 * SUB
    width = half // tiles
    rows = heads * dv
    anywhere = pl.BlockSpec(memory_space=pl.ANY)
    vmem = pl.BlockSpec(memory_space=pltpu.VMEM)
    steps = heads * SUB
    bf16, f32 = jnp.bfloat16, jnp.float32
    dma = pltpu.SemaphoreType.DMA
    return pl.pallas_call(
        functools.partial(kernel, blocks),
        out_shape=jax.ShapeDtypeStruct((length, half), bf16),
        in_specs=[anywhere, anywhere, anywhere, vmem, anywhere, vmem, anywhere],
        out_specs=anywhere,
        scratch_shapes=[
            pltpu.VMEM((length, heads * dk), bf16),
            pltpu.VMEM((length, heads * dk), bf16),
            pltpu.VMEM((length, rows), bf16),
            pltpu.VMEM((length, rows), bf16),
            pltpu.VMEM((rows, half), bf16),
            pltpu.VMEM((rows, half), bf16),
            pltpu.VMEM((heads, length, dv), bf16),
            pltpu.VMEM((heads, length, dv), bf16),
            pltpu.VMEM((tiles, length, width), f32),
            pltpu.VMEM((tiles, length, width), bf16),
            pltpu.VMEM((heads, length, dv), f32),
            pltpu.VMEM((heads * (SUB + 1), dk, dv), f32),
            pltpu.VMEM((heads, dk, dv), bf16),
            pltpu.VMEM((heads, dk, dv), bf16),
            pltpu.VMEM((heads, 1, length), f32),
            pltpu.VMEM((heads, length, 1), f32),
            pltpu.VMEM((heads, length, 1), f32),
            pltpu.VMEM((steps, 1, dv), f32),
            pltpu.VMEM((heads, 1, dv), f32),
            dma((heads,)), dma((heads,)), dma, dma, dma, dma, dma,
            dma((steps,)), dma((steps,)), dma((steps,)), dma((steps,)), dma((tiles,)),
        ],
        compiler_params=pltpu.CompilerParams(
            collective_id=0, has_side_effects=True, vmem_limit_bytes=64000 * 1024
        ),
    )(
        queries.reshape(length, heads * dk),
        keys.reshape(length, heads * dk),
        content_vectors.reshape(length, rows),
        decay_rate,
        gate_pre,
        norm_gain.reshape(1, rows),
        out_weight,
    )


def solution(mesh):
    in_specs = (
        P(("batch", "seq"), "head", None),
        P(("batch", "seq"), "head", None),
        P(("batch", "seq"), "head", None),
        P("head", ("batch", "seq")),
        P(("batch", "seq"), "head"),
        P("head"),
        P("head", None),
    )
    out_specs = P(("batch", "seq"), "head")
    return jax.shard_map(
        on_device, mesh=mesh, in_specs=in_specs, out_specs=out_specs, check_vma=False
    )
```

time: 124 us -> 64.2 us (0.52)
  Pallas kernels: 0 us -> 51.9 us
  matrix products: 32.9 us -> 0 us
  blocking collectives: 23 us -> 0 us
  waiting for transfers between devices: 20.5 us -> 0 us
  between operations: 14.1 us -> 0.01 us
  starting transfers between devices: 9.18 us -> 0 us
  other arithmetic: 8.36 us -> 0 us
  local copies, waits for them, and re-layouts: 14.8 us -> 12.1 us
    pallas_call x0 -> x1, Pallas kernels: none -> 51.9 us  [on_device(): pl.pallas_call(functools.partial(kernel, blocks), out_shape=jax.ShapeDtyp...]
    dot_general x5 -> x0, matrix products: 32.9 us -> none  [the longest x1 15 us: on_device(): jnp.dot(gated_rows, out_weight, preferred_element_type=jnp.float32)]
    unnamed x1 -> x0, blocking collectives: 23 us -> none
    reduce_scatter x1 -> x0, waiting for transfers between devices: 20 us -> none  [on_device(): lax.psum_scatter(partial_out.astype(jnp.bfloat16), 'head', scatter_dimens...]
    all_to_all x2 -> x0, starting transfers between devices: 9.18 us -> none  [the longest x1 4.65 us: transpose_prefix(): lax.all_to_all(aggregate_result.astype(jnp.bfloat16), 'seq', split_axis=1...]
    unnamed x17 -> x8, local copies, waits for them, and re-layouts: 6.03 us -> 12.1 us
    reshape x1 -> x0, local copies, waits for them, and re-layouts: 5.49 us -> none  [on_device(): (shifted * lax.rsqrt(variance + 1e-06)).reshape(length, local_heads * val...]
    mul x1 -> x0, other arithmetic: 2.54 us -> none  [on_device(): shifted * lax.rsqrt(variance + 1e-06)]
  transfers between devices with their start and end apart: 3 -> 0, of which waited for: 2 -> 0; matrix products, arithmetic and copies ran while one was open for 11% -> 0% of each run, Pallas kernels for 0% -> 0%
where the time goes in v1:
time: 64.2 us; the launch traced here: 63.9 us
  Pallas kernels  51.9 us (81%)
  local copies, waits for them, and re-layouts  12.1 us (19%)
    pallas_call x1, Pallas kernels, on_device(): pl.pallas_call(functools.partial(kernel, blocks), out_shape=jax.ShapeDtyp...  51.9 us
    unnamed x8, local copies, waits for them, and re-layouts  12.1 us

profile of v1, /device:TPU:27, one launch (start us, length us, event | category | flops | bytes accessed | tf_op | source)
XLA Modules:
  0.0 63.9 jit_solution(2336874914772321613)
XLA Ops:
  0.0 0.0 copy-start
  0.0 3.6 %copy.8 = bf16[128,8,4,256]{3,1,2,0:T(8,128)(2,1)} copy(bf16[128,8,4,256]{3,2,1,0:T(4,128)(2,1)} %bitcast.10) | data formatting | bytes 4194304
  3.6 0.0 copy-done
  3.6 0.0 copy-start.1
  3.6 1.8 %copy.9 = bf16[128,8,4,256]{3,1,2,0:T(8,128)(2,1)} copy(bf16[128,8,4,256]{3,2,1,0:T(4,128)(2,1)S(1)} %bitcast.11) | data formatting | bytes 4194304
  5.4 0.1 copy-done.1
  5.4 1.8 %copy.10 = bf16[128,8,4,256]{3,1,2,0:T(8,128)(2,1)} copy(bf16[128,8,4,256]{3,2,1,0:T(4,128)(2,1)S(1)} %bitcast.12) | data formatting | bytes 4194304
  7.3 51.9 %shard_map.73 = bf16[1024,2048]{1,0:T(8,128)(2,1)} custom-call(bf16[1024,1024]{1,0:T(8,128)(2,1)} %bitcast.7, bf16[1024,1024]{1,0:T(8,128)(2,1)} %bitcast.8, bf16[1024,1024]{1,0:T(8,128)(2,1)} %bitcast.9, f32[4,1024]{1,0:T(4,128)} %rate_ref.1, bf16[1024,1024]{1,0:T(8,128)(2,1)} %gate_hbm.1, f32[1,1024]{1,0:T(1,128)} %bitcast.13, bf16[1024,4096]{1,0:T(8,128)(2,1)} %w_hbm.1), custom_call_target="tpu_custom_call" | custom-call | tf_op jit(solution)/shard_map/pallas_call | solution.py:260
  59.2 4.8 %copy.12 = bf16[1024,2048]{1,0:T(8,128)(2,1)} copy(bf16[1024,2048]{1,0:T(8,128)(2,1)} %shard_map.73) | data formatting | bytes 8388608
Async XLA Ops:
  0.0 3.6 %copy-start = (bf16[1024,4,256]{2,1,0:T(4,128)(2,1)S(1)}, bf16[1024,4,256]{2,1,0:T(4,128)(2,1)}, u32[]{:S(2)}) copy-start(bf16[1024,4,256]{2,1,0:T(4,128)(2,1)} %param.8) | copy-start | bytes 6291460
  3.6 1.9 %copy-start.1 = (bf16[1024,4,256]{2,1,0:T(4,128)(2,1)S(1)}, bf16[1024,4,256]{2,1,0:T(4,128)(2,1)}, u32[]{:S(2)}) copy-start(bf16[1024,4,256]{2,1,0:T(4,128)(2,1)} %param.9) | copy-start | bytes 6291460

commit v2 on v1

--- a/solution.py
+++ b/solution.py
@@ -10,12 +10,12 @@
 MESH = pl.DeviceIdType.MESH
 SUB = 4
 AHEAD = 6
-LAG = 2 * SUB + 1
+GROUPS = 2
 
 
 def kernel(
     blocks, q_hbm, k_hbm, v_hbm, rate_ref, gate_hbm, gain_ref, w_hbm, out_hbm,
-    qv, kv, vv, gv, w_own, w_peer, g_own, g_peer, acc, ob, near, st, inc, sb,
+    qv, kv, vv, gv, w_all, g_all, acc, ob, near, st, inc, sb,
     wrow, wcol, ecol, fstart, ftot,
     k_sem, v_sem, q_sem, gate_sem, w_sem, ws_sem, wr_sem, ss_sem, sr_sem, gs_sem, gr_sem, o_sem,
 ):
@@ -24,9 +24,11 @@
     heads = inc.shape[0]
     rows = length // SUB
     part = dk // SUB
-    half = w_own.shape[1]
+    half = w_all.shape[2]
+    fold = heads // GROUPS
+    deep = fold * dv
     tiles, _, width = acc.shape
-    per = tiles // SUB
+    lag = SUB * (fold + 1) + 1
     s = lax.axis_index("seq")
     p = lax.axis_index("head")
 
@@ -38,14 +40,17 @@
         c = pl.ds(h * dv, dv)
         return pltpu.make_async_copy(v_hbm.at[:, c], vv.at[:, c], v_sem.at[h])
 
-    def w_local():
+    def w_local(g):
         c = pl.ds(pl.multiple_of(p * half, 128), half)
-        return pltpu.make_async_copy(w_hbm.at[:, c], w_own, w_sem)
-
-    def w_remote():
+        return pltpu.make_async_copy(
+            w_hbm.at[pl.ds(g * deep, deep), c], w_all.at[g, pl.ds(0, deep)], w_sem.at[g]
+        )
+
+    def w_remote(g):
         c = pl.ds(pl.multiple_of((1 - p) * half, 128), half)
         return pltpu.make_async_remote_copy(
-            w_hbm.at[:, c], w_peer, ws_sem, wr_sem,
+            w_hbm.at[pl.ds(g * deep, deep), c], w_all.at[g, pl.ds(deep, deep)],
+            ws_sem.at[g], wr_sem.at[g],
             device_id={"head": 1 - p}, device_id_type=MESH,
         )
 
@@ -60,8 +65,11 @@
     def g_copy(h, r):
         c = pl.ds(pl.multiple_of(r * rows, rows), rows)
         i = h * SUB + r
+        g, m = h // fold, lax.rem(h, fold)
+        here = pl.ds(pl.multiple_of(m * dv, dv), dv)
+        there = pl.ds(pl.multiple_of(deep + m * dv, dv), dv)
         return pltpu.make_async_remote_copy(
-            g_own.at[h, c], g_peer.at[h, c], gs_sem.at[i], gr_sem.at[i],
+            g_all.at[g, c, here], g_all.at[g, c, there], gs_sem.at[i], gr_sem.at[i],
             device_id={"head": 1 - p}, device_id_type=MESH,
         )
 
@@ -76,7 +84,8 @@
     gate_copy = pltpu.make_async_copy(gate_hbm, gv, gate_sem)
     q_copy.start()
     gate_copy.start()
-    w_local().start()
+    for g in range(GROUPS):
+        w_local(g).start()
 
     barrier = pltpu.get_barrier_semaphore()
     for there in (
@@ -100,7 +109,8 @@
         wcol[h] = columns[:, h : h + 1]
 
     pl.semaphore_wait(barrier, 3)
-    w_remote().start()
+    for g in range(GROUPS):
+        w_remote(g).start()
 
     @pl.when(s == 0)
     def _():
@@ -186,49 +196,41 @@
             var = jnp.mean(kept * kept, axis=1, keepdims=True)
             g = gv[t, cv].astype(jnp.float32)
             gated = kept * lax.rsqrt(var + 1e-06) * gain_ref[:, cv] * (g / (1.0 + jnp.exp(-g)))
-            g_own[h, t] = gated.astype(jnp.bfloat16)
+            here = pl.ds(pl.multiple_of(lax.rem(h, fold) * dv, dv), dv)
+            g_all[h // fold, t, here] = gated.astype(jnp.bfloat16)
             g_copy(h, r).start()
 
-        o = c - LAG
-
-        @pl.when(o == 0)
-        def _():
-            w_local().wait()
-            w_remote().wait_recv()
-
-        @pl.when((o >= 0) & (lax.rem(o, SUB) == 0))
-        def _():
-            for r in range(SUB):
-                g_copy(o // SUB, r).wait_recv()
-
-        @pl.when(o >= 0)
-        def _():
-            h = o // SUB
-            ch = pl.ds(pl.multiple_of(h * dv, dv), dv)
-            for u in range(per):
-                n = lax.rem(o, SUB) * per + u
+        o = c - lag
+
+        for g in range(GROUPS):
+
+            @pl.when(o == g * tiles)
+            def _():
+                w_local(g).wait()
+                w_remote(g).wait_recv()
+                for m in range(fold):
+                    for r in range(SUB):
+                        g_copy(g * fold + m, r).wait_recv()
+
+            @pl.when((o >= g * tiles) & (o < (g + 1) * tiles))
+            def _():
+                n = o - g * tiles
                 cn = pl.ds(pl.multiple_of(n * width, width), width)
-                total = jnp.dot(g_own[h], w_own[ch, cn], preferred_element_type=jnp.float32)
-                total += jnp.dot(g_peer[h], w_peer[ch, cn], preferred_element_type=jnp.float32)
-
-                @pl.when(h == 0)
-                def _():
+                total = jnp.dot(g_all[g], w_all[g, :, cn], preferred_element_type=jnp.float32)
+                if g > 0:
+                    total += acc[n]
+                if g < GROUPS - 1:
                     acc[n] = total
-
-                @pl.when((h > 0) & (h < heads - 1))
-                def _():
-                    acc[n] += total
-
-                @pl.when(h == heads - 1)
-                def _():
-                    ob[n] = (acc[n] + total).astype(jnp.bfloat16)
+                else:
+                    ob[n] = total.astype(jnp.bfloat16)
                     out_copy(n).start()
 
         return carry
 
-    lax.fori_loop(0, lead + steps + LAG, step, 0)
-
-    w_remote().wait_send()
+    lax.fori_loop(0, lead + lag + GROUPS * tiles, step, 0)
+
+    for g in range(GROUPS):
+        w_remote(g).wait_send()
 
     def finish(i, carry):
         g_copy(i // SUB, lax.rem(i, SUB)).wait_send()
@@ -267,10 +269,8 @@
             pltpu.VMEM((length, heads * dk), bf16),
             pltpu.VMEM((length, rows), bf16),
             pltpu.VMEM((length, rows), bf16),
-            pltpu.VMEM((rows, half), bf16),
-            pltpu.VMEM((rows, half), bf16),
-            pltpu.VMEM((heads, length, dv), bf16),
-            pltpu.VMEM((heads, length, dv), bf16),
+            pltpu.VMEM((GROUPS, 2 * rows // GROUPS, half), bf16),
+            pltpu.VMEM((GROUPS, length, 2 * rows // GROUPS), bf16),
             pltpu.VMEM((tiles, length, width), f32),
             pltpu.VMEM((tiles, length, width), bf16),
             pltpu.VMEM((heads, length, dv), f32),
@@ -282,7 +282,8 @@
             pltpu.VMEM((heads, length, 1), f32),
             pltpu.VMEM((steps, 1, dv), f32),
             pltpu.VMEM((heads, 1, dv), f32),
-            dma((heads,)), dma((heads,)), dma, dma, dma, dma, dma,
+            dma((heads,)), dma((heads,)), dma, dma,
+            dma((GROUPS,)), dma((GROUPS,)), dma((GROUPS,)),
             dma((steps,)), dma((steps,)), dma((steps,)), dma((steps,)), dma((tiles,)),
         ],
         compiler_params=pltpu.CompilerParams(

time: 64.2 us -> 52.1 us (0.81)
  Pallas kernels: 51.9 us -> 39.8 us
    pallas_call x1, Pallas kernels: 51.9 us -> 39.8 us  [on_device(): pl.pallas_call(functools.partial(kernel, blocks), out_shape=jax.ShapeDtyp...]
where the time goes in v2:
time: 52.1 us; the launch traced here: 51.9 us
  Pallas kernels  39.8 us (76%)
  local copies, waits for them, and re-layouts  12.1 us (23%)
    pallas_call x1, Pallas kernels, on_device(): pl.pallas_call(functools.partial(kernel, blocks), out_shape=jax.ShapeDtyp...  39.8 us
    unnamed x8, local copies, waits for them, and re-layouts  12.1 us

profile of v2, /device:TPU:27, one launch (start us, length us, event | category | flops | bytes accessed | tf_op | source)
XLA Modules:
  0.0 51.9 jit_solution(12450683960931259070)
XLA Ops:
  0.0 0.0 copy-start
  0.0 3.6 %copy.8 = bf16[128,8,4,256]{3,1,2,0:T(8,128)(2,1)} copy(bf16[128,8,4,256]{3,2,1,0:T(4,128)(2,1)} %bitcast.10) | data formatting | bytes 4194304
  3.6 0.0 copy-done
  3.6 0.0 copy-start.1
  3.6 1.8 %copy.9 = bf16[128,8,4,256]{3,1,2,0:T(8,128)(2,1)} copy(bf16[128,8,4,256]{3,2,1,0:T(4,128)(2,1)S(1)} %bitcast.11) | data formatting | bytes 4194304
  5.4 0.1 copy-done.1
  5.4 1.8 %copy.10 = bf16[128,8,4,256]{3,1,2,0:T(8,128)(2,1)} copy(bf16[128,8,4,256]{3,2,1,0:T(4,128)(2,1)S(1)} %bitcast.12) | data formatting | bytes 4194304
  7.3 39.8 %shard_map.73 = bf16[1024,2048]{1,0:T(8,128)(2,1)} custom-call(bf16[1024,1024]{1,0:T(8,128)(2,1)} %bitcast.7, bf16[1024,1024]{1,0:T(8,128)(2,1)} %bitcast.8, bf16[1024,1024]{1,0:T(8,128)(2,1)} %bitcast.9, f32[4,1024]{1,0:T(4,128)} %rate_ref.1, bf16[1024,1024]{1,0:T(8,128)(2,1)} %gate_hbm.1, f32[1,1024]{1,0:T(1,128)} %bitcast.13, bf16[1024,4096]{1,0:T(8,128)(2,1)} %w_hbm.1), custom_call_target="tpu_custom_call" | custom-call | tf_op jit(solution)/shard_map/pallas_call | solution.py:262
  47.1 4.8 %copy.12 = bf16[1024,2048]{1,0:T(8,128)(2,1)} copy(bf16[1024,2048]{1,0:T(8,128)(2,1)} %shard_map.73) | data formatting | bytes 8388608
Async XLA Ops:
  0.0 3.6 %copy-start = (bf16[1024,4,256]{2,1,0:T(4,128)(2,1)S(1)}, bf16[1024,4,256]{2,1,0:T(4,128)(2,1)}, u32[]{:S(2)}) copy-start(bf16[1024,4,256]{2,1,0:T(4,128)(2,1)} %param.8) | copy-start | bytes 6291460
  3.6 1.9 %copy-start.1 = (bf16[1024,4,256]{2,1,0:T(4,128)(2,1)S(1)}, bf16[1024,4,256]{2,1,0:T(4,128)(2,1)}, u32[]{:S(2)}) copy-start(bf16[1024,4,256]{2,1,0:T(4,128)(2,1)} %param.9) | copy-start | bytes 6291460

commit v3 on v2

--- a/solution.py
+++ b/solution.py
@@ -15,7 +15,7 @@
 
 def kernel(
     blocks, q_hbm, k_hbm, v_hbm, rate_ref, gate_hbm, gain_ref, w_hbm, out_hbm,
-    qv, kv, vv, gv, w_all, g_all, acc, ob, near, st, inc, sb,
+    q_raw, k_raw, v_raw, qv, kv, vv, gv, w_all, g_all, acc, ob, near, st, inc, sb,
     wrow, wcol, ecol, fstart, ftot,
     k_sem, v_sem, q_sem, gate_sem, w_sem, ws_sem, wr_sem, ss_sem, sr_sem, gs_sem, gr_sem, o_sem,
 ):
@@ -32,13 +32,18 @@
     s = lax.axis_index("seq")
     p = lax.axis_index("head")
 
-    def k_copy(h):
-        c = pl.ds(h * dk, dk)
-        return pltpu.make_async_copy(k_hbm.at[:, c], kv.at[:, c], k_sem.at[h])
-
-    def v_copy(h):
-        c = pl.ds(h * dv, dv)
-        return pltpu.make_async_copy(v_hbm.at[:, c], vv.at[:, c], v_sem.at[h])
+    k_copy = pltpu.make_async_copy(k_hbm, k_raw, k_sem)
+    v_copy = pltpu.make_async_copy(v_hbm, v_raw, v_sem)
+
+    def flatten(raw, flat):
+        fine = rows // SUB
+
+        def piece(i, carry):
+            t = pl.ds(pl.multiple_of(i * fine, fine), fine)
+            flat[t] = raw[t].reshape(fine, flat.shape[1])
+            return carry
+
+        lax.fori_loop(0, length // fine, piece, 0)
 
     def w_local(g):
         c = pl.ds(pl.multiple_of(p * half, 128), half)
@@ -77,10 +82,9 @@
         c = pl.ds(pl.multiple_of(n * width, width), width)
         return pltpu.make_async_copy(ob.at[n], out_hbm.at[:, c], o_sem.at[n])
 
-    for h in range(heads):
-        k_copy(h).start()
-        v_copy(h).start()
-    q_copy = pltpu.make_async_copy(q_hbm, qv, q_sem)
+    k_copy.start()
+    v_copy.start()
+    q_copy = pltpu.make_async_copy(q_hbm, q_raw, q_sem)
     gate_copy = pltpu.make_async_copy(gate_hbm, gv, gate_sem)
     q_copy.start()
     gate_copy.start()
@@ -116,9 +120,11 @@
     def _():
         inc[...] = jnp.zeros_like(inc)
 
+    k_copy.wait()
+    flatten(k_raw, kv)
+    v_copy.wait()
+    flatten(v_raw, vv)
     for h in range(heads):
-        k_copy(h).wait()
-        v_copy(h).wait()
         state = jnp.zeros((dk, dv), jnp.float32)
         start = jnp.zeros((1, 1), jnp.float32)
         for r in range(SUB):
@@ -145,6 +151,7 @@
                 state_copy(h, j).start()
 
     q_copy.wait()
+    flatten(q_raw, qv)
     gate_copy.wait()
     steps = heads * SUB
     lead = jnp.minimum(AHEAD * s, steps)
@@ -265,6 +272,9 @@
         in_specs=[anywhere, anywhere, anywhere, vmem, anywhere, vmem, anywhere],
         out_specs=anywhere,
         scratch_shapes=[
+            pltpu.VMEM(queries.shape, bf16),
+            pltpu.VMEM(keys.shape, bf16),
+            pltpu.VMEM(content_vectors.shape, bf16),
             pltpu.VMEM((length, heads * dk), bf16),
             pltpu.VMEM((length, heads * dk), bf16),
             pltpu.VMEM((length, rows), bf16),
@@ -282,7 +292,7 @@
             pltpu.VMEM((heads, length, 1), f32),
             pltpu.VMEM((steps, 1, dv), f32),
             pltpu.VMEM((heads, 1, dv), f32),
-            dma((heads,)), dma((heads,)), dma, dma,
+            dma, dma, dma, dma,
             dma((GROUPS,)), dma((GROUPS,)), dma((GROUPS,)),
             dma((steps,)), dma((steps,)), dma((steps,)), dma((steps,)), dma((tiles,)),
         ],
@@ -290,9 +300,9 @@
             collective_id=0, has_side_effects=True, vmem_limit_bytes=64000 * 1024
         ),
     )(
-        queries.reshape(length, heads * dk),
-        keys.reshape(length, heads * dk),
-        content_vectors.reshape(length, rows),
+        queries,
+        keys,
+        content_vectors,
         decay_rate,
         gate_pre,
         norm_gain.reshape(1, rows),

time: 52.1 us -> 47.3 us (0.908)
  local copies, waits for them, and re-layouts: 12.1 us -> 4.79 us
  Pallas kernels: 39.8 us -> 42.3 us
    unnamed x8 -> x1, local copies, waits for them, and re-layouts: 12.1 us -> 4.79 us
    pallas_call x1, Pallas kernels: 39.8 us -> 42.3 us  [on_device(): pl.pallas_call(functools.partial(kernel, blocks), out_shape=jax.ShapeDtyp...]
where the time goes in v3:
time: 47.3 us; the launch traced here: 47.1 us
  Pallas kernels  42.3 us (89%)
  local copies, waits for them, and re-layouts  4.79 us (10%)
    pallas_call x1, Pallas kernels, on_device(): pl.pallas_call(functools.partial(kernel, blocks), out_shape=jax.ShapeDtyp...  42.3 us
    unnamed x1, local copies, waits for them, and re-layouts  4.79 us

profile of v3, /device:TPU:27, one launch (start us, length us, event | category | flops | bytes accessed | tf_op | source)
XLA Modules:
  0.0 47.1 jit_solution(18015715190289529435)
XLA Ops:
  0.0 42.3 %shard_map.73 = bf16[1024,2048]{1,0:T(8,128)(2,1)} custom-call(bf16[1024,4,256]{2,1,0:T(4,128)(2,1)} %q_hbm.1, bf16[1024,4,256]{2,1,0:T(4,128)(2,1)} %k_hbm.1, bf16[1024,4,256]{2,1,0:T(4,128)(2,1)} %v_hbm.1, f32[4,1024]{1,0:T(4,128)} %rate_ref.1, bf16[1024,1024]{1,0:T(8,128)(2,1)} %gate_hbm.1, f32[1,1024]{1,0:T(1,128)} %bitcast.1, bf16[1024,4096]{1,0:T(8,128)(2,1)} %w_hbm.1), custom_call_target="tpu_custom_call" | custom-call | tf_op jit(solution)/shard_map/pallas_call | solution.py:269
  42.3 4.8 %copy.9 = bf16[1024,2048]{1,0:T(8,128)(2,1)} copy(bf16[1024,2048]{1,0:T(8,128)(2,1)} %shard_map.73) | data formatting | bytes 8388608
